TPU v7x, 32 devices: a whole 2x2x4 slice. The times are simulated.
32 devices in a mesh: gx: 2 (over x), gy: 4 (over z), gz: 4 (over y, core).
Axes of the slice: x: 2, y: 2, z: 4, core: 2. Of those that a mesh axis runs over, the one named last changes fastest.
Arguments:
- density: float32 [32, 64, 512], P('gx', 'gy', 'gz'), may hold values from 0.005 to 0.6, as said below
- coupling: float32 [14, 14], replicated, may hold values from -0.3 to 1.5, as said below
Outputs:
- potentials: float32 [14, 32, 64, 512], P(None, 'gx', 'gy', 'gz')
Inputs may be any that keep to these rules, and one draw needn't show every extreme that they name: Positive density. `coupling`: symmetric.
All inputs are finite; a program needn't handle non-finite values.
Results may differ from a plain program's by a relative error of at most 0.0003.
Values sent between devices are 32-bit elements; how exact they have to be, the bound alone decides.
A program may use at most 128 MiB of HBM per device.

v0:
```python
import math
import jax
import jax.numpy as jnp
from jax import lax
from jax.sharding import PartitionSpec as P

zab_ratio = 0.8491 / 9.0
q_cut = 5.0
mesh_step = 0.07
range_factor = 1.0
local_weight = 0.25
spline_root = math.sqrt(3.0) - 2.0
highest = lax.Precision.HIGHEST


def extended(cells, sides, width):
    for axis, dim in sides:
        count = lax.axis_size(axis)
        head = lax.slice_in_dim(cells, 0, width, axis=dim)
        tail = lax.slice_in_dim(cells, cells.shape[dim] - width, cells.shape[dim], axis=dim)
        cells = jnp.concatenate(
            [
                lax.ppermute(tail, axis, [(i, (i + 1) % count) for i in range(count)]),
                cells,
                lax.ppermute(head, axis, [((i + 1) % count, i) for i in range(count)]),
            ],
            axis=dim,
        )
    return cells


def interior(padded, dim_index, offset):
    picks = []
    for other in range(3):
        lowest = 2 + offset if other == dim_index else 2
        picks.append(slice(lowest, lowest + padded.shape[other] - 4))
    return padded[tuple(picks)]


def saturated_wavevector(density, grad_sq):
    fermi_k = jnp.cbrt(3.0 * math.pi * math.pi * density)
    reduced = grad_sq / (4.0 * fermi_k * fermi_k * density * density)
    raw_q = fermi_k * (1.0 + zab_ratio * reduced)
    scaled = raw_q / q_cut
    powered = scaled
    series = jnp.zeros_like(scaled)
    for term_order in range(1, 13):
        series = series + powered / term_order
        powered = powered * scaled
    return q_cut * (1.0 - jnp.exp(-series))


def spline_weights(q_zero, q_top, qpoints):
    position = jnp.maximum(qpoints - 1.0 + jnp.log(q_zero / q_top) / mesh_step, 0.0)
    knot_ids = jnp.arange(-1, qpoints + 1, dtype=jnp.int32)
    offset = jnp.abs(position[None, :] - knot_ids.astype(jnp.float32)[:, None])
    bspline = (
        jnp.maximum(2.0 - offset, 0.0) ** 3 - 4.0 * jnp.maximum(1.0 - offset, 0.0) ** 3
    ) / 6.0
    q_nodes = jnp.arange(qpoints, dtype=jnp.int32)
    distance = jnp.abs(knot_ids[:, None] - q_nodes[None, :])
    parity = (1 - 2 * (distance % 2)).astype(jnp.float32)
    matrix = (
        math.sqrt(3.0) * parity * jnp.exp(distance.astype(jnp.float32) * math.log(-spline_root))
    )
    return jnp.dot(matrix.T, bspline, precision=highest)


def build_thetas(dens_field, q_field, q_top, qpoints):
    weights = spline_weights(q_field.reshape(-1), q_top, qpoints)
    return (weights * dens_field.reshape(1, -1)).reshape((qpoints,) + dens_field.shape)


def join_planes(joined, count, slab_rows, groups_y, groups_z):
    size_y, size_z = (joined.shape[-2], joined.shape[-1])
    planes = joined.reshape(count, slab_rows, groups_y, groups_z, size_y, size_z)
    return planes.transpose(0, 1, 2, 4, 3, 5).reshape(
        count, slab_rows, groups_y * size_y, groups_z * size_z
    )


def wave_squared(wave_ids, length):
    folded = jnp.where(2 * wave_ids < length, wave_ids, wave_ids - length)
    wavenum = 2.0 * math.pi / length * folded.astype(jnp.float32)
    return wavenum * wavenum


def dft_tables(length):
    wave_ids = jnp.arange(length, dtype=jnp.int32)
    phases = wave_ids[:, None] * wave_ids[None, :] % length
    angles = 2.0 * math.pi / length * phases.astype(jnp.float32)
    return (jnp.cos(angles), jnp.sin(angles))


def complex_table(length, direction_sign):
    cosine, sines = dft_tables(length)
    top_row = jnp.stack([cosine, -direction_sign * sines], axis=1)
    bottom_row = jnp.stack([direction_sign * sines, cosine], axis=1)
    return jnp.stack([top_row, bottom_row], axis=0)


def forward_z(field_in):
    cosine, sines = dft_tables(field_in.shape[-1])
    matrix = jnp.stack([cosine, -sines], axis=1)
    return jnp.einsum("aryz,zpk->paryk", field_in, matrix, precision=highest)


def along_y(complex_pair, direction_sign):
    matrix = complex_table(complex_pair.shape[3], direction_sign)
    return jnp.einsum("pkqy,qaryz->parkz", matrix, complex_pair, precision=highest)


def along_x(complex_pair, direction_sign):
    matrix = complex_table(complex_pair.shape[2], direction_sign)
    return jnp.einsum("pkqx,qaxm->pakm", matrix, complex_pair, precision=highest)


def inverse_z(complex_pair):
    cosine, sines = dft_tables(complex_pair.shape[-1])
    matrix = jnp.stack([cosine, -sines], axis=0)
    return jnp.einsum("paryz,pzk->aryk", complex_pair, matrix, precision=highest)


def apply_kernel(spectra, k_squared, coupling, q_top):
    qpoints = coupling.shape[0]
    q_nodes = jnp.arange(qpoints, dtype=jnp.int32)
    q_mesh = q_top * jnp.exp(-mesh_step * (qpoints - 1 - q_nodes).astype(jnp.float32))
    masses = range_factor * q_mesh[:, None] * q_mesh[None, :]

    def add_source(source, summed):
        mass_col = lax.dynamic_index_in_dim(masses, source, 1, keepdims=False)[:, None, None]
        coupling_col = lax.dynamic_index_in_dim(coupling, source, 1, keepdims=False)[:, None, None]
        factor = coupling_col * (local_weight + mass_col / (k_squared[None] + mass_col))
        spectrum = lax.dynamic_index_in_dim(spectra, source, 1, keepdims=False)
        return summed + factor[None] * spectrum[:, None]

    return lax.fori_loop(0, qpoints, add_source, jnp.zeros_like(spectra))


def body(density, coupling):
    size_x, size_y, size_z = density.shape
    qpoints = coupling.shape[0]
    groups_x, groups_y, groups_z = (lax.axis_size("gx"), lax.axis_size("gy"), lax.axis_size("gz"))
    full_x, full_y, full_z = (size_x * groups_x, size_y * groups_y, size_z * groups_z)
    scale_inv = 1.0 / (full_x * full_y * full_z)
    padded = extended(density, (("gx", 0), ("gy", 1), ("gz", 2)), 2)
    grad_sq = jnp.zeros_like(density)
    for dim_index in range(3):
        nearer = interior(padded, dim_index, 1) - interior(padded, dim_index, -1)
        farther = interior(padded, dim_index, 2) - interior(padded, dim_index, -2)
        gradient = (8.0 * nearer - farther) / 12.0
        grad_sq = grad_sq + gradient * gradient
    q_zero = saturated_wavevector(density, grad_sq)
    q_top = lax.pmax(jnp.max(q_zero), ("gx", "gy", "gz"))
    x_waves = wave_squared(jnp.arange(full_x, dtype=jnp.int32), full_x)
    slab_rows = size_x // (groups_y * groups_z)
    thetas = build_thetas(density, q_zero, q_top, qpoints)
    joined = lax.all_to_all(
        thetas.reshape(qpoints, size_x, 1, size_y, size_z),
        ("gy", "gz"),
        split_axis=1,
        concat_axis=2,
        tiled=True,
    )
    planes = join_planes(joined, qpoints, slab_rows, groups_y, groups_z)
    spectra = along_y(forward_z(planes), -1.0)
    plane_part = full_y * full_z // (groups_x * groups_y * groups_z)
    xlines = lax.all_to_all(
        spectra.reshape(2, qpoints, slab_rows, full_y * full_z),
        ("gx", "gy", "gz"),
        split_axis=3,
        concat_axis=2,
        tiled=True,
    )
    flat_index = lax.axis_index(("gx", "gy", "gz")) * plane_part + jnp.arange(
        plane_part, dtype=jnp.int32
    )
    k_squared = (
        x_waves[:, None]
        + (wave_squared(flat_index // full_z, full_y) + wave_squared(flat_index % full_z, full_z))[
            None, :
        ]
    )
    products = along_x(apply_kernel(along_x(xlines, -1.0), k_squared, coupling, q_top), 1.0)
    returned = lax.all_to_all(
        products, ("gx", "gy", "gz"), split_axis=2, concat_axis=3, tiled=True
    ).reshape(2, qpoints, slab_rows, full_y, full_z)
    fields = inverse_z(along_y(returned, 1.0)) * scale_inv
    spread = fields.reshape(qpoints, slab_rows, groups_y, size_y, groups_z, size_z)
    spread = spread.transpose(0, 1, 2, 4, 3, 5).reshape(
        qpoints, slab_rows, groups_y * groups_z, size_y, size_z
    )
    blocks = lax.all_to_all(spread, ("gy", "gz"), split_axis=2, concat_axis=1, tiled=True)
    return blocks.reshape(qpoints, size_x, size_y, size_z)


def solution(mesh):
    placed = (P("gx", "gy", "gz"), P())
    return jax.shard_map(
        body, mesh=mesh, in_specs=placed, out_specs=P(None, "gx", "gy", "gz"), check_vma=False
    )
```

profile of v0, /device:TPU:1, one launch (start us, length us, event | category | flops | bytes accessed | tf_op | source)
XLA Modules:
  0.0 683.4 jit_solution(6947540007924352375)
XLA Ops:
  18.2 6.7 collective-permute-done.4
  26.1 36.2 %pmax.7 = f32[]{:T(128)} all-reduce(f32[]{:T(128)} %get-tuple-element.178), channel_id=1, replica_groups=mesh['gx'=2,'gy'=4,'gz'=4] {'gx','gy','gz'}, use_global_device_ids=true, to_apply=%region_1.0 | all-reduce | flops 1 | bytes 8 | tf_op jit(solution)/shard_map/pmax | solution.py:154
  67.5 7.5 %all-to-all-start = ((f32[14,16,1,16,128]{4,3,0,2,1:T(8,128)}), f32[14,16,1,16,128]{4,3,0,2,1:T(8,128)S(1)}, u32[]{:S(2)}, u32[]{:S(2)}) async-start(f32[14,16,1,16,128]{4,3,0,2,1:T(8,128)} %copy.18), calls=%async_computation | async-start | bytes 3670016 | tf_op jit(solution)/shard_map/all_to_all | solution.py:158
  75.3 5.3 sine_negate_fusion.1
  80.6 31.4 %all-to-all-done = f32[14,16,1,16,128]{4,3,0,2,1:T(8,128)S(1)} async-done(((f32[14,16,1,16,128]{4,3,0,2,1:T(8,128)}), f32[14,16,1,16,128]{4,3,0,2,1:T(8,128)S(1)}, u32[]{:S(2)}, u32[]{:S(2)}) %all-to-all-start) | async-done | bytes 1835040 | tf_op jit(solution)/shard_map/all_to_all | solution.py:158
  116.6 7.6 %fusion.28 = f32[2,14,64,512,1]{3,2,1,0,4:T(8,128)S(1)} fusion(f32[14,64,512,1]{2,1,0,3:T(8,128)S(1)} %reshape.462, f32[512,1,512]{2,0,1:T(8,128)S(1)} %get-tuple-element.209, f32[512,1,512]{2,0,1:T(8,128)} %get-tuple-element.210), kind=kOutput, calls=%fused_computation.36 | convolution fusion | flops 5637668864 | bytes 7602176 | tf_op jit(solution)/shard_map/aryz,zpk->paryk/dot_general | solution.py:105
  124.2 5.8 fusion.29
  130.0 26.4 %copy.41 = f32[2,14,1,64,512]{1,0,4,3,2:T(2,128)} copy(f32[2,14,1,64,512]{4,3,0,1,2:T(8,128)} %fusion.29) | data formatting | bytes 7340032 | tf_op jit(solution)/shard_map/reshape | solution.py:169
  156.4 56.7 %reshape.479 = f32[32,1,28672]{2,1,0:T(1,128)} reshape(f32[32768,1,2,14]{3,2,1,0:T(2,128)} %bitcast.123) | data formatting | bytes 7340032
  213.1 9.2 %all-to-all-start.1 = ((f32[32,1,28672]{2,1,0:T(1,128)}), f32[32,1,28672]{2,1,0:T(1,128)}, u32[]{:S(2)}, u32[]{:S(2)}) async-start(f32[32,1,28672]{2,1,0:T(1,128)} %reshape.479), calls=%async_computation.1 | async-start | bytes 7340032 | tf_op jit(solution)/shard_map/all_to_all | solution.py:168
  223.3 81.8 %all-to-all-done.1 = f32[32,1,28672]{2,1,0:T(1,128)} async-done(((f32[32,1,28672]{2,1,0:T(1,128)}), f32[32,1,28672]{2,1,0:T(1,128)}, u32[]{:S(2)}, u32[]{:S(2)}) %all-to-all-start.1) | async-done | bytes 3670048 | tf_op jit(solution)/shard_map/all_to_all | solution.py:168
  305.7 12.8 %reduce = f32[32,28672]{1,0:T(8,128)} reduce(f32[32,1,28672]{2,1,0:T(1,128)} %all-to-all-done.1, f32[]{:T(128)} %broadcast.803), dimensions={1}, to_apply=%all_to_all.11.reduce_sub_computation | reduce | bytes 7340036 | tf_op jit(solution)/shard_map/all_to_all | solution.py:168
  318.5 72.2 %reshape.480 = f32[32768,1,2,14]{3,2,1,0:T(2,128)} reshape(f32[32,28672]{1,0:T(8,128)} %reduce) | data formatting | bytes 7340032
  390.7 28.0 %copy.32 = f32[2,14,32,1024,1]{3,2,0,4,1:T(8,128)} copy(f32[2,14,32,1024,1]{1,0,3,2,4:T(2,128)} %bitcast.124) | data formatting | bytes 7340032 | tf_op jit(solution)/shard_map/all_to_all | solution.py:168
  418.7 6.4 convolution_bitcast_fusion
  425.2 85.2 %while.14 = (s32[]{:T(128)}, f32[2,14,32,1024]{3,2,1,0:T(8,128)}, f32[14,14]{0,1:T(8,128)S(1)}, f32[14,14]{0,1:T(8,128)S(1)}, f32[2,14,32,1024]{3,2,0,1:T(8,128)...) while((s32[]{:T(128)}, f32[2,14,32,1024]{3,2,1,0:T(8,128)}, ...), condition=%wide.region_3.4_spmd.clone, body=%wide.region_2.3_spmd.clone.sunk | while | flops 4620291 | bytes 12063295 | solution.py:137
  431.2 4.8 select_add_fusion.2
  510.4 6.6 fusion.32
  530.2 78.8 %all-to-all-done.2 = f32[2,14,32,1024]{3,0,1,2:T(2,128)} async-done(((f32[2,14,32,1024]{3,0,1,2:T(2,128)}), f32[2,14,32,1024]{3,0,1,2:T(2,128)}, u32[]{:S(2)}, u32[]{:S(2)}) %all-to-all-start.2) | async-done | bytes 3670048 | tf_op jit(solution)/shard_map/all_to_all | solution.py:185
  609.0 6.0 copy.26
  615.1 4.9 reshape.472
  620.0 6.0 fusion.6
  626.0 7.1 %bitcast_multiply_fusion = f32[14,64,512]{2,1,0:T(8,128)} fusion(f32[1,512,512]{2,1,0:T(8,128)S(1)} %get-tuple-element.215, f32[1,512,512]{2,1,0:T(8,128)S(1)} %get-tuple-element.216, f32[14,512,2,64,1]{1,3,4,2,0:T(8,128)S(1)} %fusion.6), kind=kOutput, calls=%fused_computation.40 | convolution fusion | flops 5638127616 | bytes 7602176 | tf_op jit(solution)/shard_map/paryz,pzk->aryk/dot_general | solution.py:121
  635.2 46.6 %all_to_all.19 = f32[14,1,16,16,128]{4,3,0,1,2:T(8,128)S(1)} all-to-all(f32[14,1,16,16,128]{4,3,0,1,2:T(8,128)S(1)} %bitcast.130), channel_id=1, replica_groups=mesh['gx'=2,'gy'=4,'gz'=4] {'gy','gz'}, dimensions={2} | all-to-all | bytes 3670016 | tf_op jit(solution)/shard_map/all_to_all | solution.py:193
  (119 shorter events, 127.4 us)
Async XLA Ops:
  0.0 24.9 %copy-start = (f32[16,16,128]{2,1,0:T(8,128)S(1)}, f32[16,16,128]{2,1,0:T(8,128)}, u32[]{:S(2)}) copy-start(f32[16,16,128]{2,1,0:T(8,128)} %param.4) | copy-start | bytes 393220
  0.8 3.2 collective-permute-start.1
  2.8 2.6 collective-permute-start
  5.4 4.6 collective-permute-start.2
  9.1 4.4 collective-permute-start.3
  13.7 11.2 %collective-permute-start.4 = (f32[20,20,2]{2,1,0:T(8,128)S(1)}, f32[20,20,2]{2,1,0:T(8,128)S(1)}, u32[]{:S(2)}, u32[]{:S(2)}) collective-permute-start(f32[20,20,2]{2,1,0:T(8,128)S(1)} %get-tuple-element.182), channel_id=1, source_target_pairs={{1,0},{2,1},{3,2},{0,3},{5,4},{6,5},{7,6},{4,7},{9,8},{10,9},{11,1... | collective-permute-start | bytes 9608 | tf_op jit(solution)/shard_map/ppermute | solution.py:25
  17.0 7.9 %collective-permute-start.5 = (f32[20,20,2]{2,1,0:T(8,128)S(1)}, f32[20,20,2]{2,1,0:T(8,128)S(1)}, u32[]{:S(2)}, u32[]{:S(2)}) collective-permute-start(f32[20,20,2]{2,1,0:T(8,128)S(1)} %get-tuple-element.183), channel_id=1, source_target_pairs={{0,1},{1,2},{2,3},{3,0},{4,5},{5,6},{6,7},{7,4},{8,9},{9,10},{10,1... | collective-permute-start | bytes 9608 | tf_op jit(solution)/shard_map/ppermute | solution.py:23
  67.5 44.4 %all-to-all-start = ((f32[14,16,1,16,128]{4,3,0,2,1:T(8,128)}), f32[14,16,1,16,128]{4,3,0,2,1:T(8,128)S(1)}, u32[]{:S(2)}, u32[]{:S(2)}) async-start(f32[14,16,1,16,128]{4,3,0,2,1:T(8,128)} %copy.18), calls=%async_computation | async-start | bytes 3670016 | tf_op jit(solution)/shard_map/all_to_all | solution.py:158
  213.1 9.2 %copy-start.1 = (f32[14,14]{1,0:T(8,128)S(1)}, f32[14,14]{1,0:T(8,128)}, u32[]{:S(2)}) copy-start(f32[14,14]{1,0:T(8,128)} %param.5) | copy-start | bytes 2356
  213.1 92.0 %all-to-all-start.1 = ((f32[32,1,28672]{2,1,0:T(1,128)}), f32[32,1,28672]{2,1,0:T(1,128)}, u32[]{:S(2)}, u32[]{:S(2)}) async-start(f32[32,1,28672]{2,1,0:T(1,128)} %reshape.479), calls=%async_computation.1 | async-start | bytes 7340032 | tf_op jit(solution)/shard_map/all_to_all | solution.py:168
  521.7 87.4 %all-to-all-start.2 = ((f32[2,14,32,1024]{3,0,1,2:T(2,128)}), f32[2,14,32,1024]{3,0,1,2:T(2,128)}, u32[]{:S(2)}, u32[]{:S(2)}) async-start(f32[2,14,32,1024]{3,0,1,2:T(2,128)} %copy.25), calls=%async_computation.2 | async-start | bytes 7340032 | tf_op jit(solution)/shard_map/all_to_all | solution.py:185
where the time goes:
time: 693 us; the launch traced here: 683 us
  local copies, waits for them, and re-layouts  225 us (32%)
  waiting for transfers between devices  205 us (30%)
  other arithmetic  96 us (14%)
  blocking collectives  82.7 us (12%)
  matrix products  42.2 us (6%)
  starting transfers between devices  31.3 us (5%)
    unnamed x11, local copies, waits for them, and re-layouts  130 us
    all_to_all x1, waiting for transfers between devices, body(): lax.all_to_all(spectra.reshape(2, qpoints, slab_rows, full_y * full_z), (...  81.8 us
    all_to_all x1, waiting for transfers between devices, body(): lax.all_to_all(products, ('gx', 'gy', 'gz'), split_axis=2, concat_axis=3,...  78.8 us
    add x14, other arithmetic, add_source(): return summed + factor[None] * spectrum[:, None]  64.5 us
    all_to_all x1, blocking collectives, body(): lax.all_to_all(spread, ('gy', 'gz'), split_axis=2, concat_axis=1, tiled=T...  46.6 us
    pmax x1, blocking collectives, body(): q_top = lax.pmax(jnp.max(q_zero), ('gx', 'gy', 'gz'))  36.2 us
    all_to_all x1, waiting for transfers between devices, body(): lax.all_to_all(thetas.reshape(qpoints, size_x, 1, size_y, size_z), ('gy',...  31.4 us
    all_to_all x2, local copies, waits for them, and re-layouts, body(): lax.all_to_all(spectra.reshape(2, qpoints, slab_rows, full_y * full_z), (...  28.6 us
  transfers between devices with their start and end apart: 9, of which 8 were waited for; matrix products, arithmetic and copies ran while one was open for 2% of the time, Pallas kernels for 0%

commit v1 on v0

--- a/solution.py
+++ b/solution.py
@@ -182,8 +182,14 @@
         ]
     )
     products = along_x(apply_kernel(along_x(xlines, -1.0), k_squared, coupling, q_top), 1.0)
-    returned = lax.all_to_all(
-        products, ("gx", "gy", "gz"), split_axis=2, concat_axis=3, tiled=True
+    returned = jnp.concatenate(
+        lax.all_to_all(
+            jnp.stack(jnp.split(products, lax.axis_size(("gx", "gy", "gz")), axis=2)),
+            ("gx", "gy", "gz"),
+            0,
+            0,
+        ),
+        axis=3,
     ).reshape(2, qpoints, slab_rows, full_y, full_z)
     fields = inverse_z(along_y(returned, 1.0)) * scale_inv
     spread = fields.reshape(qpoints, slab_rows, groups_y, size_y, groups_z, size_z)

time: 693 us -> 716 us (1.033)
  local copies, waits for them, and re-layouts: 225 us -> 246 us
    unnamed x11 -> x42, local copies, waits for them, and re-layouts: 130 us -> 152 us
where the time goes in v1:
time: 716 us; the launch traced here: 706 us
  local copies, waits for them, and re-layouts  246 us (34%)
  waiting for transfers between devices  205 us (29%)
  other arithmetic  97.2 us (14%)
  blocking collectives  82.8 us (12%)
  matrix products  42.2 us (6%)
  starting transfers between devices  31.3 us (4%)
    unnamed x42, local copies, waits for them, and re-layouts  152 us
    all_to_all x1, waiting for transfers between devices, body(): lax.all_to_all(spectra.reshape(2, qpoints, slab_rows, full_y * full_z), (...  81.7 us
    all_to_all x1, waiting for transfers between devices, body(): lax.all_to_all(jnp.stack(jnp.split(products, lax.axis_size(('gx', 'gy', '...  78.8 us
    add x14, other arithmetic, add_source(): return summed + factor[None] * spectrum[:, None]  64.6 us
    all_to_all x1, blocking collectives, body(): lax.all_to_all(spread, ('gy', 'gz'), split_axis=2, concat_axis=1, tiled=T...  46.6 us
    pmax x1, blocking collectives, body(): q_top = lax.pmax(jnp.max(q_zero), ('gx', 'gy', 'gz'))  36.2 us
    all_to_all x1, waiting for transfers between devices, body(): lax.all_to_all(thetas.reshape(qpoints, size_x, 1, size_y, size_z), ('gy',...  31.4 us
    all_to_all x2, local copies, waits for them, and re-layouts, body(): lax.all_to_all(spectra.reshape(2, qpoints, slab_rows, full_y * full_z), (...  28.6 us
  transfers between devices with their start and end apart: 9, of which 8 were waited for; matrix products, arithmetic and copies ran while one was open for 2% of the time, Pallas kernels for 0%

profile of v1, /device:TPU:1, one launch (start us, length us, event | category | flops | bytes accessed | tf_op | source)
XLA Modules:
  0.0 705.9 jit_solution(17958896206293218751)
XLA Ops:
  18.2 6.7 collective-permute-done.4
  27.1 36.2 %pmax.7 = f32[]{:T(128)} all-reduce(f32[]{:T(128)} %get-tuple-element.185), channel_id=1, replica_groups=mesh['gx'=2,'gy'=4,'gz'=4] {'gx','gy','gz'}, use_global_device_ids=true, to_apply=%region_1.0 | all-reduce | flops 1 | bytes 8 | tf_op jit(solution)/shard_map/pmax | solution.py:154
  68.7 7.5 %all-to-all-start = ((f32[14,16,1,16,128]{4,3,0,2,1:T(8,128)}), f32[14,16,1,16,128]{4,3,0,2,1:T(8,128)S(1)}, u32[]{:S(2)}, u32[]{:S(2)}) async-start(f32[14,16,1,16,128]{4,3,0,2,1:T(8,128)} %copy.119), calls=%async_computation | async-start | bytes 3670016 | tf_op jit(solution)/shard_map/all_to_all | solution.py:158
  76.5 5.3 sine_negate_fusion.1
  81.8 31.4 %all-to-all-done = f32[14,16,1,16,128]{4,3,0,2,1:T(8,128)S(1)} async-done(((f32[14,16,1,16,128]{4,3,0,2,1:T(8,128)}), f32[14,16,1,16,128]{4,3,0,2,1:T(8,128)S(1)}, u32[]{:S(2)}, u32[]{:S(2)}) %all-to-all-start) | async-done | bytes 1835040 | tf_op jit(solution)/shard_map/all_to_all | solution.py:158
  117.7 7.6 %fusion.28 = f32[2,14,64,512,1]{3,2,1,0,4:T(8,128)S(1)} fusion(f32[14,64,512,1]{2,1,0,3:T(8,128)S(1)} %reshape.461, f32[512,1,512]{2,0,1:T(8,128)S(1)} %get-tuple-element.248, f32[512,1,512]{2,0,1:T(8,128)} %get-tuple-element.249), kind=kOutput, calls=%fused_computation.36 | convolution fusion | flops 5637668864 | bytes 7602176 | tf_op jit(solution)/shard_map/aryz,zpk->paryk/dot_general | solution.py:105
  125.3 5.8 fusion.29
  131.1 26.5 %copy.173 = f32[2,14,1,64,512]{1,0,4,3,2:T(2,128)} copy(f32[2,14,1,64,512]{4,3,0,1,2:T(8,128)} %fusion.29) | data formatting | bytes 7340032 | tf_op jit(solution)/shard_map/reshape | solution.py:169
  157.6 56.7 %reshape.479 = f32[32,1,28672]{2,1,0:T(1,128)} reshape(f32[32768,1,2,14]{3,2,1,0:T(2,128)} %bitcast.250) | data formatting | bytes 7340032
  214.3 9.2 %all-to-all-start.1 = ((f32[32,1,28672]{2,1,0:T(1,128)}), f32[32,1,28672]{2,1,0:T(1,128)}, u32[]{:S(2)}, u32[]{:S(2)}) async-start(f32[32,1,28672]{2,1,0:T(1,128)} %reshape.479), calls=%async_computation.1 | async-start | bytes 7340032 | tf_op jit(solution)/shard_map/all_to_all | solution.py:168
  224.6 81.7 %all-to-all-done.1 = f32[32,1,28672]{2,1,0:T(1,128)} async-done(((f32[32,1,28672]{2,1,0:T(1,128)}), f32[32,1,28672]{2,1,0:T(1,128)}, u32[]{:S(2)}, u32[]{:S(2)}) %all-to-all-start.1) | async-done | bytes 3670048 | tf_op jit(solution)/shard_map/all_to_all | solution.py:168
  306.9 12.8 %reduce = f32[32,28672]{1,0:T(8,128)} reduce(f32[32,1,28672]{2,1,0:T(1,128)} %all-to-all-done.1, f32[]{:T(128)} %broadcast.803), dimensions={1}, to_apply=%all_to_all.11.reduce_sub_computation | reduce | bytes 7340036 | tf_op jit(solution)/shard_map/all_to_all | solution.py:168
  319.7 72.2 %reshape.480 = f32[32768,1,2,14]{3,2,1,0:T(2,128)} reshape(f32[32,28672]{1,0:T(8,128)} %reduce) | data formatting | bytes 7340032
  391.9 28.0 %copy.164 = f32[2,14,32,1024,1]{3,2,0,4,1:T(8,128)} copy(f32[2,14,32,1024,1]{1,0,3,2,4:T(2,128)} %bitcast.251) | data formatting | bytes 7340032 | tf_op jit(solution)/shard_map/all_to_all | solution.py:168
  419.9 6.5 convolution_bitcast_fusion
  426.3 85.3 %while.14 = (s32[]{:T(128)}, f32[2,14,32,1024]{3,2,1,0:T(8,128)}, f32[14,14]{0,1:T(8,128)S(1)}, f32[14,14]{0,1:T(8,128)S(1)}, f32[2,14,32,1024]{3,2,0,1:T(8,128)...) while((s32[]{:T(128)}, f32[2,14,32,1024]{3,2,1,0:T(8,128)}, ...), condition=%wide.region_3.4_spmd.clone, body=%wide.region_2.3_spmd.clone.sunk | while | flops 4620291 | bytes 12063295 | solution.py:137
  432.4 4.8 select_add_fusion.2
  511.6 6.6 fusion.32
  552.7 78.8 %all-to-all-done.2 = f32[32,2,14,1,1024]{4,1,2,3,0:T(2,128)} async-done(((f32[32,2,14,1,1024]{4,1,2,3,0:T(2,128)}), f32[32,2,14,1,1024]{4,1,2,3,0:T(2,128)}, u32[]{:S(2)}, u32[]{:S(2)}) %all-to-all-start.2) | async-done | bytes 3670048 | tf_op jit(solution)/shard_map/all_to_all | solution.py:186
  631.6 6.0 copy.179
  637.6 5.0 reshape.471
  642.5 6.0 fusion.6
  648.5 7.1 %bitcast_multiply_fusion = f32[14,64,512]{2,1,0:T(8,128)} fusion(f32[1,512,512]{2,1,0:T(8,128)S(1)} %get-tuple-element.254, f32[1,512,512]{2,1,0:T(8,128)S(1)} %get-tuple-element.255, f32[14,512,2,64,1]{1,3,4,2,0:T(8,128)S(1)} %fusion.6), kind=kOutput, calls=%fused_computation.40 | convolution fusion | flops 5638127616 | bytes 7602176 | tf_op jit(solution)/shard_map/paryz,pzk->aryk/dot_general | solution.py:121
  657.7 46.6 %all_to_all.35 = f32[14,1,16,16,128]{4,3,0,1,2:T(8,128)S(1)} all-to-all(f32[14,1,16,16,128]{4,3,0,1,2:T(8,128)S(1)} %bitcast.257), channel_id=1, replica_groups=mesh['gx'=2,'gy'=4,'gz'=4] {'gy','gz'}, dimensions={2} | all-to-all | bytes 3670016 | tf_op jit(solution)/shard_map/all_to_all | solution.py:199
  (152 shorter events, 149.9 us)
Async XLA Ops:
  0.0 64.0 %copy-start = (f32[16,16,128]{2,1,0:T(8,128)S(1)}, f32[16,16,128]{2,1,0:T(8,128)}, u32[]{:S(2)}) copy-start(f32[16,16,128]{2,1,0:T(8,128)} %param.4) | copy-start | bytes 393220
  0.8 3.2 collective-permute-start.1
  2.8 2.6 collective-permute-start
  5.4 4.6 collective-permute-start.2
  9.1 4.4 collective-permute-start.3
  13.7 11.2 %collective-permute-start.4 = (f32[20,20,2]{2,1,0:T(8,128)S(1)}, f32[20,20,2]{2,1,0:T(8,128)S(1)}, u32[]{:S(2)}, u32[]{:S(2)}) collective-permute-start(f32[20,20,2]{2,1,0:T(8,128)S(1)} %get-tuple-element.221), channel_id=1, source_target_pairs={{1,0},{2,1},{3,2},{0,3},{5,4},{6,5},{7,6},{4,7},{9,8},{10,9},{11,1... | collective-permute-start | bytes 9608 | tf_op jit(solution)/shard_map/ppermute | solution.py:25
  17.0 7.9 %collective-permute-start.5 = (f32[20,20,2]{2,1,0:T(8,128)S(1)}, f32[20,20,2]{2,1,0:T(8,128)S(1)}, u32[]{:S(2)}, u32[]{:S(2)}) collective-permute-start(f32[20,20,2]{2,1,0:T(8,128)S(1)} %get-tuple-element.222), channel_id=1, source_target_pairs={{0,1},{1,2},{2,3},{3,0},{4,5},{5,6},{6,7},{7,4},{8,9},{9,10},{10,1... | collective-permute-start | bytes 9608 | tf_op jit(solution)/shard_map/ppermute | solution.py:23
  68.7 44.4 %all-to-all-start = ((f32[14,16,1,16,128]{4,3,0,2,1:T(8,128)}), f32[14,16,1,16,128]{4,3,0,2,1:T(8,128)S(1)}, u32[]{:S(2)}, u32[]{:S(2)}) async-start(f32[14,16,1,16,128]{4,3,0,2,1:T(8,128)} %copy.119), calls=%async_computation | async-start | bytes 3670016 | tf_op jit(solution)/shard_map/all_to_all | solution.py:158
  214.3 9.3 %copy-start.1 = (f32[14,14]{1,0:T(8,128)S(1)}, f32[14,14]{1,0:T(8,128)}, u32[]{:S(2)}) copy-start(f32[14,14]{1,0:T(8,128)} %param.5) | copy-start | bytes 2356
  214.3 92.1 %all-to-all-start.1 = ((f32[32,1,28672]{2,1,0:T(1,128)}), f32[32,1,28672]{2,1,0:T(1,128)}, u32[]{:S(2)}, u32[]{:S(2)}) async-start(f32[32,1,28672]{2,1,0:T(1,128)} %reshape.479), calls=%async_computation.1 | async-start | bytes 7340032 | tf_op jit(solution)/shard_map/all_to_all | solution.py:168
  544.2 87.4 %all-to-all-start.2 = ((f32[32,2,14,1,1024]{4,1,2,3,0:T(2,128)}), f32[32,2,14,1,1024]{4,1,2,3,0:T(2,128)}, u32[]{:S(2)}, u32[]{:S(2)}) async-start(f32[32,2,14,1,1024]{4,1,2,3,0:T(2,128)} %bitcast_dynamic-update-slice_fusion), calls=%async_computation.2 | async-start | bytes 7340032 | tf_op jit(solution)/shard_map/all_to_all | solution.py:186
